TPU v7x, 32 devices: a whole 2x2x4 slice. The times are simulated.
32 devices in a mesh: gx: 4 (over y, x), gy: 4 (over z), gz: 2 (over core).
Axes of the slice: x: 2, y: 2, z: 4, core: 2. Of those that a mesh axis runs over, the one named last changes fastest.
Arguments:
- seg_rows: bfloat16 [4096, 128, 128], P(('gx', 'gy', 'gz')), may hold values from -6 to 6
- owner_map: int32 [4096, 1], replicated, may hold values from 0 to 31; in each aligned block of 128 rows (0 to 127, 128 to 255, ...) at most 8 rows name the same one
- ghost_pick: int32 [32, 1], P(('gx', 'gy', 'gz')), may hold values from 0 to 127
- slab_cost: int32 [4, 4, 2, 3, 1024], P('gx', 'gy', 'gz'), may hold values from 1 to 24
Outputs:
- forces: bfloat16 [32, 32, 8, 128, 128], P(('gx', 'gy', 'gz'))
- cut_points: float32 [7], replicated
Inputs may be any that keep to these rules, and one draw needn't show every extreme that they name: `owner_map`: among the 128 blocks of one device (aligned runs of 128 rows) no owner is named more than 8 times; some device names some owner exactly 8 times.
All inputs are finite; a program needn't handle non-finite values.
Results may differ from a plain program's by a relative error of at most 0.0034.
Values may be sent and summed in bfloat16 or wider, within the bound.
A program may use at most 128 MiB of HBM per device.

v0:
```python
import math
import jax
import jax.numpy as jnp
from jax import lax
from jax.sharding import PartitionSpec as P

sharpness = 8.0
force_gain = 2.0
radius_eps = 0.001


def padded_2(cells, sides, width):
    for axis, dim in sides:
        count = lax.axis_size(axis)
        head = lax.slice_in_dim(cells, 0, width, axis=dim)
        tail = lax.slice_in_dim(cells, cells.shape[dim] - width, cells.shape[dim], axis=dim)
        cells = jnp.concatenate(
            [
                lax.ppermute(tail, axis, [(i, (i + 1) % count) for i in range(count)]),
                cells,
                lax.ppermute(head, axis, [((i + 1) % count, i) for i in range(count)]),
            ],
            axis=dim,
        )
    return cells


def bisect_cuts(histogram):
    running = jnp.cumsum(histogram, axis=1, dtype=jnp.int32)
    total_cost = running[:, -1]
    below = (2 * running < total_cost[:, None]).astype(jnp.int32)
    position = jnp.sum(below, axis=1, dtype=jnp.int32)
    before = jnp.sum(histogram * below, axis=1, dtype=jnp.int32)
    bins_index = lax.broadcasted_iota(jnp.int32, histogram.shape, 1)
    at_cut = jnp.sum(
        jnp.where(bins_index == position[:, None], histogram, 0), axis=1, dtype=jnp.int32
    )
    remain = (total_cost - 2 * before).astype(jnp.float32)
    return (
        position.astype(jnp.float32) + remain / (2 * at_cut).astype(jnp.float32)
    ) / histogram.shape[1]


def kernel_weights(left_sq, right_sq, inner):
    spread = left_sq + right_sq - 2.0 * inner
    return jnp.exp(-sharpness * spread / (left_sq + right_sq + radius_eps)).astype(jnp.bfloat16)


def pair_forces(slot_rows, ghost_set, ghost_sq):
    rows_f = slot_rows.astype(jnp.float32)
    own_sq = jnp.sum(rows_f * rows_f, axis=-1)
    own_inner = jnp.einsum("sbw,scw->sbc", slot_rows, slot_rows, preferred_element_type=jnp.float32)
    ghost_inner = jnp.einsum(
        "sbw,mw->sbm", slot_rows, ghost_set, preferred_element_type=jnp.float32
    )
    own_kernel = kernel_weights(own_sq[:, :, None], own_sq[:, None, :], own_inner)
    ghost_kernel = kernel_weights(own_sq[:, :, None], ghost_sq[None, None, :], ghost_inner)
    weight_sum = jnp.sum(own_kernel.astype(jnp.float32), axis=-1) + jnp.sum(
        ghost_kernel.astype(jnp.float32), axis=-1
    )
    pulled = jnp.einsum("sbc,scw->sbw", own_kernel, slot_rows, preferred_element_type=jnp.float32)
    pulled = pulled + jnp.einsum(
        "sbm,mw->sbw", ghost_kernel, ghost_set, preferred_element_type=jnp.float32
    )
    return (force_gain * (pulled - weight_sum[..., None] * rows_f)).astype(jnp.bfloat16)


def per_device(seg_rows, owner_map, ghost_pick, slab_cost):
    count_x = lax.axis_size("gx")
    count_y = lax.axis_size("gy")
    count_z = lax.axis_size("gz")
    device_count = count_x * count_y * count_z
    blocks_here, block_rows, width = seg_rows.shape
    capacity = max(2, (2 * blocks_here + device_count - 1) // device_count)
    own_index = lax.axis_index(("gx", "gy", "gz"))
    index_x = lax.axis_index("gx")
    index_y = lax.axis_index("gy")
    local_cost = slab_cost[0, 0, 0]
    bins_count = local_cost.shape[1]
    half_part = index_x // (count_x // 2)
    quarter = half_part * 2 + index_y // (count_y // 2)
    x_term = local_cost[0][None]
    y_term = jnp.where(
        lax.broadcasted_iota(jnp.int32, (2, bins_count), 0) == half_part, local_cost[1][None], 0
    )
    z_term = jnp.where(
        lax.broadcasted_iota(jnp.int32, (4, bins_count), 0) == quarter, local_cost[2][None], 0
    )
    histogram = lax.psum(jnp.concatenate([x_term, y_term, z_term], axis=0), ("gx", "gy", "gz"))
    extent = jnp.array([count_x, count_y, count_y, count_z, count_z, count_z, count_z], jnp.float32)
    cut_points = bisect_cuts(histogram) * extent
    exported = jnp.take(seg_rows, ghost_pick[0], axis=0)
    padded = padded_2(exported[None, None, None], (("gx", 0), ("gy", 1), ("gz", 2)), 1)
    ghost_set = jnp.concatenate(
        [
            padded[0, 1, 1],
            padded[2, 1, 1],
            padded[1, 0, 1],
            padded[1, 2, 1],
            padded[1, 1, 0],
            padded[1, 1, 2],
        ],
        axis=0,
    ).reshape(-1, width)
    ghost_float = ghost_set.astype(jnp.float32)
    ghost_sq = jnp.sum(ghost_float * ghost_float, axis=-1)
    all_owners = owner_map[:, 0].reshape(device_count, blocks_here)
    own_owners = lax.dynamic_index_in_dim(all_owners, own_index, 0, keepdims=False)
    block_order = lax.broadcasted_iota(jnp.int32, (blocks_here,), 0)
    earlier = block_order[:, None] < block_order[None, :]
    same_owner = own_owners[:, None] == own_owners[None, :]
    slot_rank = jnp.sum((same_owner & earlier).astype(jnp.int32), axis=0, dtype=jnp.int32)
    slot_of = own_owners * capacity + slot_rank
    slot_ids = lax.broadcasted_iota(jnp.int32, (device_count * capacity,), 0)
    matches = slot_of[None, :] == slot_ids[:, None]
    source_block = jnp.sum(jnp.where(matches, block_order[None, :], 0), axis=1, dtype=jnp.int32)
    filled = jnp.any(matches, axis=1)
    outgoing = jnp.where(
        filled[:, None, None], jnp.take(seg_rows, source_block, axis=0), jnp.zeros((), jnp.bfloat16)
    )
    outgoing = outgoing.reshape(device_count, capacity, block_rows, width)
    arrivals = jnp.sum((all_owners == own_index).astype(jnp.int32), axis=1, dtype=jnp.int32)
    valid_slot = lax.broadcasted_iota(jnp.int32, (device_count, capacity), 1) < arrivals[:, None]
    received = lax.all_to_all(outgoing, ("gx", "gy", "gz"), split_axis=0, concat_axis=0, tiled=True)
    flat_slots = received.reshape(-1, block_rows, width)
    slot_total = flat_slots.shape[0]
    group_size = math.gcd(slot_total, 16)
    grouped = flat_slots.reshape(slot_total // group_size, group_size, block_rows, width)
    settled = lax.map(lambda piece: pair_forces(piece, ghost_set, ghost_sq), grouped)
    forces = settled.reshape(received.shape)
    forces = jnp.where(valid_slot[:, :, None, None], forces, jnp.zeros((), jnp.bfloat16))
    return (forces[None], cut_points)


def solution(mesh):
    return jax.shard_map(
        per_device,
        mesh=mesh,
        in_specs=(
            P(("gx", "gy", "gz"), None, None),
            P(),
            P(("gx", "gy", "gz"), None),
            P("gx", "gy", "gz", None, None),
        ),
        out_specs=(P(("gx", "gy", "gz"), None, None, None, None), P()),
        check_vma=False,
    )
```

profile of v0, /device:TPU:0, one launch (start us, length us, event | category | flops | bytes accessed | tf_op | source)
XLA Modules:
  0.0 430.7 jit_solution(12656038109581809656)
XLA Ops:
  2.6 10.8 %gather_fusion = bf16[256,128,128]{2,1,0:T(8,128)(2,1)} fusion(bf16[128,128,128]{2,1,0:T(8,128)(2,1)} %param.7, s32[1024]{0:T(1024)S(1)} %pad_clamp_fusion), kind=kCustom, calls=%fused_computation | custom fusion | bytes 16778240 | tf_op jit(solution)/shard_map/jit(_take)/gather | solution.py:119
  13.4 7.4 %select_select_fusion = bf16[32,8,128,128]{3,2,1,0:T(8,128)(2,1)} fusion(bf16[32,8,128,128]{3,2,1,0:T(8,128)(2,1)} %bitcast.108, pred[32,8]{1,0:T(8,128)(4,1)S(1)} %compare_and_fusion, pred[32,8]{1,0:T(8,128)(4,1)S(1)} %broadcast_in_dim.117), kind=kLoop, calls=%fused_computation.37 | loop fusion | flops 8388608 | bytes 16777728 | tf_op jit(solution)/shard_map/jit(_where)/select_n | solution.py:118
  20.8 7.5 %all-to-all-start = ((bf16[32,8,128,128]{3,2,1,0:T(8,128)(2,1)}), bf16[32,8,128,128]{3,2,1,0:T(8,128)(2,1)}, u32[]{:S(2)}, u32[]{:S(2)}) async-start(bf16[32,8,128,128]{3,2,1,0:T(8,128)(2,1)} %select_select_fusion), calls=%async_computation | async-start | bytes 16777216 | tf_op jit(solution)/shard_map/all_to_all | solution.py:124
  32.8 199.1 %psum.7 = s32[7,1024]{1,0:T(8,128)S(1)} all-reduce(s32[7,1024]{1,0:T(8,128)S(1)} %pad_add_fusion), channel_id=1, replica_groups=mesh['gx'=4,'gy'=4,'gz'=2] {'gx','gy','gz'}, use_global_device_ids=true, to_apply=%region_10.11 | all-reduce | flops 7168 | bytes 57344 | tf_op jit(solution)/shard_map/psum | solution.py:89
  236.1 3.8 collective-permute-start.3
  239.9 2.9 collective-permute-done.2
  245.1 178.2 %while.11 = (s32[]{:T(128)}, bf16[16,16,128,128]{3,2,1,0:T(8,128)(2,1)}, bf16[16,16,128,128]{3,2,1,0:T(8,128)(2,1)}, f32[768]{0:T(1024)S(1)}, bf16[768,128]{1,0:T(8,128)(2,1)S(1)}, /*index=5*/s32[]{:T(128)}) while((s32[]{:T(128)}, bf16[16,16,128,128]{3,2,1,0:T(8,128)(2,1)}, bf16[16,16,128,128]{3,2,1,0:T(8,128)(2,1)}, f32[768]{0:T(1024)S(1)}, ...), condition=%wide.region_9.10_spmd, body=%wide.region_5.9_spmd.sunk | while | flops 958394368 | bytes 13063241 | solution.py:129
  246.5 3.5 convert_reduce_fusion.8
  253.4 2.9 fusion.50
  257.6 3.5 convert_reduce_fusion.8
  268.8 3.5 convert_reduce_fusion.8
  279.9 3.5 convert_reduce_fusion.8
  286.8 2.9 fusion.50
  291.0 3.5 convert_reduce_fusion.8
  302.1 3.5 convert_reduce_fusion.8
  313.3 3.5 convert_reduce_fusion.8
  320.1 2.9 fusion.50
  324.4 3.5 convert_reduce_fusion.8
  335.5 3.5 convert_reduce_fusion.8
  342.4 2.9 fusion.50
  346.6 3.5 convert_reduce_fusion.8
  353.5 2.9 fusion.50
  357.8 3.5 convert_reduce_fusion.8
  368.9 3.5 convert_reduce_fusion.8
  375.8 2.9 fusion.50
  380.0 3.5 convert_reduce_fusion.8
  391.2 3.5 convert_reduce_fusion.8
  398.1 2.9 fusion.50
  402.4 3.5 convert_reduce_fusion.8
  413.5 3.5 convert_reduce_fusion.8
  420.4 2.9 fusion.50
  423.3 7.4 %broadcast_select_fusion = bf16[1,32,8,128,128]{4,3,2,1,0:T(8,128)(2,1)} fusion(bf16[1,32,8,128,128]{4,3,2,1,0:T(8,128)(2,1)} %bitcast.23, pred[32,8]{1,0:T(8,128)(4,1)S(1)} %iota_compare_fusion.3), kind=kLoop, calls=%fused_computation.38 | loop fusion | flops 4194304 | bytes 16777472 | tf_op jit(solution)/shard_map/jit(_where)/select_n | solution.py:131
  (129 shorter events, 111.1 us)
Async XLA Ops:
  20.8 11.8 %copy-start.1 = (s32[1,1,1,3,1024]{4,2,3,1,0:T(1,128)S(1)}, s32[1,1,1,3,1024]{4,2,3,1,0:T(1,128)}, u32[]{:S(2)}) copy-start(s32[1,1,1,3,1024]{4,2,3,1,0:T(1,128)} %param.10) | copy-start | bytes 36868
  20.8 213.9 %copy-start = (s32[4096,1]{0,1:T(1,128)S(1)}, s32[4096,1]{0,1:T(1,128)}, u32[]{:S(2)}) copy-start(s32[4096,1]{0,1:T(1,128)} %param.8) | copy-start | bytes 49156
  20.8 214.6 %copy-start.2 = (f32[7]{0:T(128)S(1)}, f32[7]{0:T(128)}, u32[]{:S(2)}) copy-start(f32[7]{0:T(128)} %constant.111.clone) | copy-start | bytes 88
  20.8 224.3 %all-to-all-start = ((bf16[32,8,128,128]{3,2,1,0:T(8,128)(2,1)}), bf16[32,8,128,128]{3,2,1,0:T(8,128)(2,1)}, u32[]{:S(2)}, u32[]{:S(2)}) async-start(bf16[32,8,128,128]{3,2,1,0:T(8,128)(2,1)} %select_select_fusion), calls=%async_computation | async-start | bytes 16777216 | tf_op jit(solution)/shard_map/all_to_all | solution.py:124
  29.7 206.3 %collective-permute-start = (bf16[1,1,1,1,128,128]{5,4,3,2,1,0:T(8,128)(2,1)S(1)}, bf16[1,1,1,1,128,128]{5,4,3,2,1,0:T(8,128)(2,1)S(1)}, u32[]{:S(2)}, u32[]{:S(2)}) collective-permute-start(bf16[1,1,1,1,128,128]{5,4,3,2,1,0:T(8,128)(2,1)S(1)} %fusion.32), channel_id=1, source_target_pairs={{0,8},{8,16},{16,24},{24,0},{1,9},{9,17},{17,25},{25,1},{2,10},{10... | collective-permute-start | bytes 98312 | tf_op jit(solution)/shard_map/ppermute | solution.py:19
  31.4 204.6 %collective-permute-start.1 = (bf16[1,1,1,1,128,128]{5,4,3,2,1,0:T(8,128)(2,1)S(1)}, bf16[1,1,1,1,128,128]{5,4,3,2,1,0:T(8,128)(2,1)S(1)}, u32[]{:S(2)}, u32[]{:S(2)}) collective-permute-start(bf16[1,1,1,1,128,128]{5,4,3,2,1,0:T(8,128)(2,1)S(1)} %fusion.32), channel_id=1, source_target_pairs={{8,0},{16,8},{24,16},{0,24},{9,1},{17,9},{25,17},{1,25},{10,2},{18... | collective-permute-start | bytes 98312 | tf_op jit(solution)/shard_map/ppermute | solution.py:21
  236.0 6.8 %collective-permute-start.2 = (bf16[3,1,1,1,128,128]{5,4,3,2,1,0:T(8,128)(2,1)S(1)}, bf16[3,1,1,1,128,128]{5,4,3,2,1,0:T(8,128)(2,1)S(1)}, u32[]{:S(2)}, u32[]{:S(2)}) collective-permute-start(bf16[3,1,1,1,128,128]{5,4,3,2,1,0:T(8,128)(2,1)S(1)} %pad_maximum_fusion.1), channel_id=1, source_target_pairs={{0,2},{2,4},{4,6},{6,0},{1,3},{3,5},{5,7},{7,1},{8,10},{10,12},{12... | collective-permute-start | bytes 294920 | tf_op jit(solution)/shard_map/ppermute | solution.py:19
  236.1 6.7 %collective-permute-start.3 = (bf16[3,1,1,1,128,128]{5,4,3,2,1,0:T(8,128)(2,1)S(1)}, bf16[3,1,1,1,128,128]{5,4,3,2,1,0:T(8,128)(2,1)S(1)}, u32[]{:S(2)}, u32[]{:S(2)}) collective-permute-start(bf16[3,1,1,1,128,128]{5,4,3,2,1,0:T(8,128)(2,1)S(1)} %pad_maximum_fusion.1), channel_id=1, source_target_pairs={{2,0},{4,2},{6,4},{0,6},{3,1},{5,3},{7,5},{1,7},{10,8},{12,10},{14... | collective-permute-start | bytes 294920 | tf_op jit(solution)/shard_map/ppermute | solution.py:21
  242.8 1.6 collective-permute-start.4
  242.9 2.0 collective-permute-start.5
where the time goes:
time: 435 us; the launch traced here: 431 us
  blocking collectives  199 us (46%)
  matrix products  155 us (36%)
  other arithmetic  42.7 us (10%)
  starting transfers between devices  14.8 us (3%)
  local copies, waits for them, and re-layouts  12.2 us (3%)
  waiting for transfers between devices  4.39 us (1%)
    psum x1, blocking collectives, per_device(): lax.psum(jnp.concatenate([x_term, y_term, z_term], axis=0), ('gx', 'gy',...  199 us
    dot_general x16, matrix products, pair_forces(): jnp.einsum('sbw,mw->sbm', slot_rows, ghost_set, preferred_element_type=jn...  55.7 us
    dot_general x16, matrix products, pair_forces(): jnp.einsum('sbm,mw->sbw', ghost_kernel, ghost_set, preferred_element_type...  46 us
    dot_general x16, matrix products, pair_forces(): jnp.einsum('sbw,scw->sbc', slot_rows, slot_rows, preferred_element_type=j...  32.2 us
    reduce_sum x16, other arithmetic, pair_forces(): own_sq = jnp.sum(rows_f * rows_f, axis=-1)  22.1 us
    dot_general x16, matrix products, pair_forces(): jnp.einsum('sbc,scw->sbw', own_kernel, slot_rows, preferred_element_type=...  21.6 us
    gather x1, local copies, waits for them, and re-layouts, per_device(): jnp.take(seg_rows, source_block, axis=0)  10.8 us
  transfers between devices with their start and end apart: 7, of which 3 were waited for; matrix products, arithmetic and copies ran while one was open for 1% of the time, Pallas kernels for 0%

commit v1 on v0

--- a/solution.py
+++ b/solution.py
@@ -7,6 +7,12 @@
 sharpness = 8.0
 force_gain = 2.0
 radius_eps = 0.001
+
+
+def sources_all_serve(unit):
+    oldest = lax.all_gather(unit, ("gx", "gy", "gz"))
+    m_next = jnp.sum(oldest, 0)
+    return m_next
 
 
 def padded_2(cells, sides, width):
@@ -86,7 +92,7 @@
     z_term = jnp.where(
         lax.broadcasted_iota(jnp.int32, (4, bins_count), 0) == quarter, local_cost[2][None], 0
     )
-    histogram = lax.psum(jnp.concatenate([x_term, y_term, z_term], axis=0), ("gx", "gy", "gz"))
+    histogram = sources_all_serve(jnp.concatenate([x_term, y_term, z_term], axis=0))
     extent = jnp.array([count_x, count_y, count_y, count_z, count_z, count_z, count_z], jnp.float32)
     cut_points = bisect_cuts(histogram) * extent
     exported = jnp.take(seg_rows, ghost_pick[0], axis=0)

time: 435 us -> 450 us (1.034)
  blocking collectives: 199 us -> 214 us
    all_gather x0 -> x1, blocking collectives: none -> 214 us  [sources_all_serve(): oldest = lax.all_gather(unit, ('gx', 'gy', 'gz'))]
    psum x1 -> x0, blocking collectives: 199 us -> none  [per_device(): lax.psum(jnp.concatenate([x_term, y_term, z_term], axis=0), ('gx', 'gy',...]
where the time goes in v1:
time: 450 us; the launch traced here: 446 us
  blocking collectives  214 us (48%)
  matrix products  155 us (34%)
  other arithmetic  42.8 us (10%)
  starting transfers between devices  14.8 us (3%)
  local copies, waits for them, and re-layouts  12.2 us (3%)
  waiting for transfers between devices  5.1 us (1%)
    all_gather x1, blocking collectives, sources_all_serve(): oldest = lax.all_gather(unit, ('gx', 'gy', 'gz'))  214 us
    dot_general x16, matrix products, pair_forces(): jnp.einsum('sbw,mw->sbm', slot_rows, ghost_set, preferred_element_type=jn...  55.7 us
    dot_general x16, matrix products, pair_forces(): jnp.einsum('sbm,mw->sbw', ghost_kernel, ghost_set, preferred_element_type...  46 us
    dot_general x16, matrix products, pair_forces(): jnp.einsum('sbw,scw->sbc', slot_rows, slot_rows, preferred_element_type=j...  32.2 us
    reduce_sum x16, other arithmetic, pair_forces(): own_sq = jnp.sum(rows_f * rows_f, axis=-1)  22.1 us
    dot_general x16, matrix products, pair_forces(): jnp.einsum('sbc,scw->sbw', own_kernel, slot_rows, preferred_element_type=...  21.6 us
    gather x1, local copies, waits for them, and re-layouts, per_device(): jnp.take(seg_rows, source_block, axis=0)  10.8 us
  transfers between devices with their start and end apart: 7, of which 3 were waited for; matrix products, arithmetic and copies ran while one was open for 1% of the time, Pallas kernels for 0%

profile of v1, /device:TPU:0, one launch (start us, length us, event | category | flops | bytes accessed | tf_op | source)
XLA Modules:
  0.0 446.1 jit_solution(5421681048913256312)
XLA Ops:
  2.6 10.8 %gather_fusion = bf16[256,128,128]{2,1,0:T(8,128)(2,1)} fusion(bf16[128,128,128]{2,1,0:T(8,128)(2,1)} %param.7, s32[1024]{0:T(1024)S(1)} %pad_clamp_fusion), kind=kCustom, calls=%fused_computation | custom fusion | bytes 16778240 | tf_op jit(solution)/shard_map/jit(_take)/gather | solution.py:125
  13.4 7.4 %select_select_fusion = bf16[32,8,128,128]{3,2,1,0:T(8,128)(2,1)} fusion(bf16[32,8,128,128]{3,2,1,0:T(8,128)(2,1)} %bitcast.110, pred[32,8]{1,0:T(8,128)(4,1)S(1)} %compare_and_fusion, pred[32,8]{1,0:T(8,128)(4,1)S(1)} %broadcast_in_dim.117), kind=kLoop, calls=%fused_computation.37 | loop fusion | flops 8388608 | bytes 16777728 | tf_op jit(solution)/shard_map/jit(_where)/select_n | solution.py:124
  20.8 7.5 %all-to-all-start = ((bf16[32,8,128,128]{3,2,1,0:T(8,128)(2,1)}), bf16[32,8,128,128]{3,2,1,0:T(8,128)(2,1)}, u32[]{:S(2)}, u32[]{:S(2)}) async-start(bf16[32,8,128,128]{3,2,1,0:T(8,128)(2,1)} %select_select_fusion), calls=%async_computation | async-start | bytes 16777216 | tf_op jit(solution)/shard_map/all_to_all | solution.py:130
  32.8 213.7 %all-gather.1 = s32[32,7,1024]{2,1,0:T(8,128)S(1)} all-gather(s32[1,7,1024]{2,1,0:T(8,128)S(1)} %add_bitcast_fusion), channel_id=2, replica_groups=mesh['gx'=4,'gy'=4,'gz'=2] {'gx','gy','gz'}, dimensions={0}, use_global_device_ids=true | all-gather | bytes 946176 | tf_op jit(solution)/shard_map/all_gather | solution.py:13
  250.7 3.8 collective-permute-start.3
  254.6 3.6 collective-permute-done.2
  260.5 178.1 %while.11 = (s32[]{:T(128)}, bf16[16,16,128,128]{3,2,1,0:T(8,128)(2,1)}, bf16[16,16,128,128]{3,2,1,0:T(8,128)(2,1)}, f32[768]{0:T(1024)S(1)}, bf16[768,128]{1,0:T(8,128)(2,1)S(1)}, /*index=5*/s32[]{:T(128)}) while((s32[]{:T(128)}, bf16[16,16,128,128]{3,2,1,0:T(8,128)(2,1)}, bf16[16,16,128,128]{3,2,1,0:T(8,128)(2,1)}, f32[768]{0:T(1024)S(1)}, ...), condition=%wide.region_9.10_spmd, body=%wide.region_5.9_spmd.sunk | while | flops 958394368 | bytes 13063241 | solution.py:135
  261.9 3.5 convert_reduce_fusion.8
  268.8 2.9 fusion.50
  273.0 3.5 convert_reduce_fusion.8
  284.1 3.5 convert_reduce_fusion.8
  295.3 3.5 convert_reduce_fusion.8
  302.1 2.9 fusion.50
  306.4 3.5 convert_reduce_fusion.8
  313.3 2.9 fusion.50
  317.5 3.5 convert_reduce_fusion.8
  328.7 3.5 convert_reduce_fusion.8
  339.8 3.5 convert_reduce_fusion.8
  350.9 3.5 convert_reduce_fusion.8
  357.8 2.9 fusion.50
  362.0 3.5 convert_reduce_fusion.8
  368.9 2.9 fusion.50
  373.1 3.5 convert_reduce_fusion.8
  384.3 3.5 convert_reduce_fusion.8
  391.1 2.9 fusion.50
  395.4 3.5 convert_reduce_fusion.8
  406.5 3.5 convert_reduce_fusion.8
  413.5 2.9 fusion.50
  417.8 3.5 convert_reduce_fusion.8
  428.9 3.5 convert_reduce_fusion.8
  435.8 2.9 fusion.50
  438.6 7.4 %broadcast_select_fusion = bf16[1,32,8,128,128]{4,3,2,1,0:T(8,128)(2,1)} fusion(bf16[1,32,8,128,128]{4,3,2,1,0:T(8,128)(2,1)} %bitcast.23, pred[32,8]{1,0:T(8,128)(4,1)S(1)} %iota_compare_fusion.3), kind=kLoop, calls=%fused_computation.38 | loop fusion | flops 4194304 | bytes 16777472 | tf_op jit(solution)/shard_map/jit(_where)/select_n | solution.py:137
  (130 shorter events, 111.2 us)
Async XLA Ops:
  20.8 11.8 %copy-start.1 = (s32[1,1,1,3,1024]{4,2,3,1,0:T(1,128)S(1)}, s32[1,1,1,3,1024]{4,2,3,1,0:T(1,128)}, u32[]{:S(2)}) copy-start(s32[1,1,1,3,1024]{4,2,3,1,0:T(1,128)} %param.10) | copy-start | bytes 36868
  20.8 228.6 %copy-start = (s32[4096,1]{0,1:T(1,128)S(1)}, s32[4096,1]{0,1:T(1,128)}, u32[]{:S(2)}) copy-start(s32[4096,1]{0,1:T(1,128)} %param.8) | copy-start | bytes 49156
  20.8 229.3 %copy-start.2 = (f32[7]{0:T(128)S(1)}, f32[7]{0:T(128)}, u32[]{:S(2)}) copy-start(f32[7]{0:T(128)} %constant.111.clone) | copy-start | bytes 88
  20.8 239.7 %all-to-all-start = ((bf16[32,8,128,128]{3,2,1,0:T(8,128)(2,1)}), bf16[32,8,128,128]{3,2,1,0:T(8,128)(2,1)}, u32[]{:S(2)}, u32[]{:S(2)}) async-start(bf16[32,8,128,128]{3,2,1,0:T(8,128)(2,1)} %select_select_fusion), calls=%async_computation | async-start | bytes 16777216 | tf_op jit(solution)/shard_map/all_to_all | solution.py:130
  29.7 220.9 %collective-permute-start = (bf16[1,1,1,1,128,128]{5,4,3,2,1,0:T(8,128)(2,1)S(1)}, bf16[1,1,1,1,128,128]{5,4,3,2,1,0:T(8,128)(2,1)S(1)}, u32[]{:S(2)}, u32[]{:S(2)}) collective-permute-start(bf16[1,1,1,1,128,128]{5,4,3,2,1,0:T(8,128)(2,1)S(1)} %fusion.32), channel_id=1, source_target_pairs={{0,8},{8,16},{16,24},{24,0},{1,9},{9,17},{17,25},{25,1},{2,10},{10... | collective-permute-start | bytes 98312 | tf_op jit(solution)/shard_map/ppermute | solution.py:25
  31.4 219.3 %collective-permute-start.1 = (bf16[1,1,1,1,128,128]{5,4,3,2,1,0:T(8,128)(2,1)S(1)}, bf16[1,1,1,1,128,128]{5,4,3,2,1,0:T(8,128)(2,1)S(1)}, u32[]{:S(2)}, u32[]{:S(2)}) collective-permute-start(bf16[1,1,1,1,128,128]{5,4,3,2,1,0:T(8,128)(2,1)S(1)} %fusion.32), channel_id=1, source_target_pairs={{8,0},{16,8},{24,16},{0,24},{9,1},{17,9},{25,17},{1,25},{10,2},{18... | collective-permute-start | bytes 98312 | tf_op jit(solution)/shard_map/ppermute | solution.py:27
  250.7 7.5 %collective-permute-start.2 = (bf16[3,1,1,1,128,128]{5,4,3,2,1,0:T(8,128)(2,1)S(1)}, bf16[3,1,1,1,128,128]{5,4,3,2,1,0:T(8,128)(2,1)S(1)}, u32[]{:S(2)}, u32[]{:S(2)}) collective-permute-start(bf16[3,1,1,1,128,128]{5,4,3,2,1,0:T(8,128)(2,1)S(1)} %pad_maximum_fusion.1), channel_id=1, source_target_pairs={{0,2},{2,4},{4,6},{6,0},{1,3},{3,5},{5,7},{7,1},{8,10},{10,12},{12... | collective-permute-start | bytes 294920 | tf_op jit(solution)/shard_map/ppermute | solution.py:25
  250.7 7.5 %collective-permute-start.3 = (bf16[3,1,1,1,128,128]{5,4,3,2,1,0:T(8,128)(2,1)S(1)}, bf16[3,1,1,1,128,128]{5,4,3,2,1,0:T(8,128)(2,1)S(1)}, u32[]{:S(2)}, u32[]{:S(2)}) collective-permute-start(bf16[3,1,1,1,128,128]{5,4,3,2,1,0:T(8,128)(2,1)S(1)} %pad_maximum_fusion.1), channel_id=1, source_target_pairs={{2,0},{4,2},{6,4},{0,6},{3,1},{5,3},{7,5},{1,7},{10,8},{12,10},{14... | collective-permute-start | bytes 294920 | tf_op jit(solution)/shard_map/ppermute | solution.py:27
  258.2 1.6 collective-permute-start.4
  258.3 2.0 collective-permute-start.5
